TPU v7x, 32 devices: a whole 2x2x4 slice. The times are simulated.
32 devices in a mesh: rows: 8 (over z, x), cols: 4 (over y, core).
Axes of the slice: x: 2, y: 2, z: 4, core: 2. Of those that a mesh axis runs over, the one named last changes fastest.
Arguments:
- basis: bfloat16 [65536, 512], P('rows', 'cols'), may hold values from -6 to 6
- lower: bfloat16 [256, 256, 256], P('rows'), may hold values from -0.375 to 0.375
- diag: bfloat16 [256, 256, 256], P('rows'), may hold values from -0.375 to 0.375
- upper: bfloat16 [256, 256, 256], P('rows'), may hold values from -0.375 to 0.375
- inverse: bfloat16 [256, 256, 256], P('rows'), may hold values from -0.375 to 0.375
Outputs:
- ortho: bfloat16 [65536, 512], P('rows', 'cols')
- projected: float32 [512, 512], P(None, 'cols')
All inputs are finite; a program needn't handle non-finite values.
Results may differ from a plain program's by a relative error of at most 0.0085.
Values may be sent and summed in bfloat16 or wider, within the bound.
A program may use at most 128 MiB of HBM per device.

v0:
```python
import jax
import jax.numpy as jnp
from jax import lax
from jax.sharding import PartitionSpec as P


def extended(block, sides, width):
    for axis, dim in sides:
        count = lax.axis_size(axis)
        forward = [(i, i + 1) for i in range(count - 1)]
        backward = [(target, source) for source, target in forward]
        low = lax.ppermute(
            lax.slice_in_dim(block, block.shape[dim] - width, None, axis=dim), axis, forward
        )
        high = lax.ppermute(lax.slice_in_dim(block, 0, width, axis=dim), axis, backward)
        block = jnp.concatenate([low, block, high], axis=dim)
    return block


def inner(left, right):
    return lax.dot_general(
        left, right, (((0,), (0,)), ((), ())), preferred_element_type=jnp.float32
    )


def apply_blocks(padded, lower, diag, upper, inverse):
    count = diag.shape[0]
    size = diag.shape[1]
    width = padded.shape[1]
    blocks = padded.reshape(count + 2, size, width)
    mixed = jnp.einsum("bij,bjc->bic", lower, blocks[:-2], preferred_element_type=jnp.float32)
    mixed = mixed + jnp.einsum(
        "bij,bjc->bic", diag, blocks[1:-1], preferred_element_type=jnp.float32
    )
    mixed = mixed + jnp.einsum(
        "bij,bjc->bic", upper, blocks[2:], preferred_element_type=jnp.float32
    )
    mixed = mixed.astype(jnp.bfloat16)
    result = jnp.einsum("bij,bjc->bic", inverse, mixed, preferred_element_type=jnp.float32)
    return result.astype(jnp.bfloat16).reshape(count * size, width)


def inverse_upper(gram):
    factor = jnp.linalg.cholesky(gram)
    identity = jnp.eye(gram.shape[0], dtype=jnp.float32)
    linv = lax.linalg.triangular_solve(factor, identity, left_side=True, lower=True)
    return linv.T.astype(jnp.bfloat16)


def shards(basis, lower, diag, upper, inverse):
    size = diag.shape[1]
    width = basis.shape[1]

    def operate(field):
        padded = extended(field, (("rows", 0),), size)
        return apply_blocks(padded, lower, diag, upper, inverse)

    work = operate(basis)
    wide = lax.all_gather(work, "cols", axis=1, tiled=True)
    gram = lax.psum(inner(wide, wide), "rows")
    rinv = inverse_upper(gram)
    start = lax.axis_index("cols") * width
    ortho_all = jnp.dot(wide, rinv, preferred_element_type=jnp.float32).astype(jnp.bfloat16)
    ortho = lax.dynamic_slice_in_dim(ortho_all, start, width, 1)
    image = operate(ortho)
    projected = lax.psum(inner(ortho_all, image), "rows")
    return (ortho, projected)


def solution(mesh):
    in_specs = (
        P("rows", "cols"),
        P("rows", None, None),
        P("rows", None, None),
        P("rows", None, None),
        P("rows", None, None),
    )
    out_specs = (P("rows", "cols"), P(None, "cols"))
    return jax.shard_map(shards, mesh=mesh, in_specs=in_specs, out_specs=out_specs, check_vma=False)
```

profile of v0, /device:TPU:0, one launch (start us, length us, event | category | flops | bytes accessed | tf_op | source)
XLA Modules:
  0.0 457.5 jit_solution(3944854083608453380)
XLA Ops:
  9.4 5.5 %collective-permute-start = (bf16[256,128]{1,0:T(8,128)(2,1)S(1)}, bf16[256,128]{1,0:T(8,128)(2,1)S(1)}, u32[]{:S(2)}, u32[]{:S(2)}) collective-permute-start(bf16[256,128]{1,0:T(8,128)(2,1)S(1)} %get-tuple-element.27), channel_id=1, source_target_pairs={{0,4},{4,8},{8,12},{12,16},{16,20},{20,24},{24,28},{1,5},{5,9},{9,... | collective-permute-start | bytes 196616 | tf_op jit(solution)/shard_map/ppermute | solution.py:12
  14.9 6.5 %fusion.49 = f32[32,256,128]{1,2,0:T(8,128)} fusion(bf16[32,256,256]{2,1,0:T(8,128)(2,1)} %param.7, bf16[32,256,128]{2,1,0:T(8,128)(2,1)} %bitcast.98), kind=kOutput, calls=%fused_computation.97 | convolution fusion | flops 536870912 | bytes 10485760 | tf_op jit(solution)/shard_map/bij,bjc->bic/dot_general | solution.py:32
  21.7 1.9 copy-done.2
  23.6 3.5 fusion.48
  27.0 10.1 %convert_bitcast_fusion.1 = bf16[32,256,128]{1,2,0:T(8,128)(2,1)} fusion(bf16[32,256,256]{2,1,0:T(8,128)(2,1)} %param.9, f32[32,256,128]{1,2,0:T(8,128)} %fusion.49, f32[32,128,256]{2,1,0:T(8,128)} %fusion.48, bf16[32,256,128]{2,1,0:T(8,128)(2,1)S(1)} %bitcast.99, bf16[32,256,256]{2,1,0:T(8,128)(2,1)} %param.8), kind=kOutput, calls=%fused_computation.14 | convolution fusion | flops 1077936128 | bytes 20971520 | tf_op jit(solution)/shard_map/bij,bjc->bic/dot_general | solution.py:39
  37.1 4.0 copy.9
  41.2 61.1 %all-gather.2.cloned.1.call-done = bf16[8192,512]{1,0:T(8,128)(2,1)} async-done(((bf16[8192,128]{1,0:T(8,128)(2,1)}), bf16[8192,512]{1,0:T(8,128)(2,1)}) %all-gather.2.cloned.1.call-update) | async-done | bytes 8388624 | tf_op jit(solution)/shard_map/all_gather | solution.py:59
  102.4 11.3 %fusion.50 = f32[512,512]{0,1:T(8,128)} fusion(bf16[8192,512]{1,0:T(8,128)(2,1)} %all-gather.2.cloned.1.call-done), kind=kOutput, calls=%fused_computation.98 | convolution fusion | flops 4294967296 | bytes 9437184 | tf_op jit(solution)/shard_map/dot_general | solution.py:21
  114.8 77.2 %all-reduce.4.cloned.1.call-done = f32[512,512]{0,1:T(8,128)} async-done(((f32[512,512]{0,1:T(8,128)}), f32[512,512]{0,1:T(8,128)}) %all-reduce.4.cloned.1.call-update) | async-done | bytes 1048592 | tf_op jit(solution)/shard_map/psum | solution.py:60
  195.1 11.7 %cholesky.104 = f32[128,128]{1,0:T(8,128)S(1)} custom-call(f32[128,128]{1,0:T(8,128)S(1)} %cholesky.266), custom_call_target="Cholesky" | custom-call | tf_op jit(solution)/shard_map/jit(cholesky)/cholesky | solution.py:44
  206.8 9.8 %custom-call.30 = f32[1,128,128]{1,2,0:T(8,128)S(1)} custom-call(f32[1,128,128]{2,1,0:T(8,128)S(1)} %get-tuple-element.37), custom_call_target="InvertDiagBlocksLowerTriangular" | custom-call | tf_op jit(solution)/shard_map/jit(cholesky)/cholesky | solution.py:44
  217.4 11.7 %cholesky.217 = f32[128,128]{1,0:T(8,128)S(1)} custom-call(f32[128,128]{1,0:T(8,128)S(1)} %cholesky.270), custom_call_target="Cholesky" | custom-call | tf_op jit(solution)/shard_map/jit(cholesky)/cholesky | solution.py:44
  229.2 10.0 %custom-call.31 = f32[1,128,128]{1,2,0:T(8,128)S(1)} custom-call(f32[1,128,128]{2,1,0:T(8,128)S(1)} %get-tuple-element.34), custom_call_target="InvertDiagBlocksLowerTriangular" | custom-call | tf_op jit(solution)/shard_map/jit(cholesky)/cholesky | solution.py:44
  239.8 11.7 %cholesky.238 = f32[128,128]{1,0:T(8,128)S(1)} custom-call(f32[128,128]{1,0:T(8,128)S(1)} %cholesky.275), custom_call_target="Cholesky" | custom-call | tf_op jit(solution)/shard_map/jit(cholesky)/cholesky | solution.py:44
  252.3 9.8 %custom-call.32 = f32[1,128,128]{1,2,0:T(8,128)S(1)} custom-call(f32[1,128,128]{2,1,0:T(8,128)S(1)} %get-tuple-element.31), custom_call_target="InvertDiagBlocksLowerTriangular" | custom-call | tf_op jit(solution)/shard_map/jit(cholesky)/cholesky | solution.py:44
  262.7 11.7 %cholesky.255 = f32[128,128]{1,0:T(8,128)S(1)} custom-call(f32[128,128]{1,0:T(8,128)S(1)} %convolution_subtract_fusion.5), custom_call_target="Cholesky" | custom-call | tf_op jit(solution)/shard_map/jit(cholesky)/cholesky | solution.py:44
  278.9 10.8 %while.1 = (s32[]{:T(128)}, f32[512,512]{1,0:T(8,128)S(1)}, s32[4,2]{0,1:T(2,128)S(1)}, f32[4,128,128]{2,1,0:T(8,128)}, s32[]{:T(128)}) while((s32[]{:T(128)}, f32[512,512]{1,0:T(8,128)S(1)}, s32[4,2]{0,1:T(2,128)S(1)}, f32[4,128,128]{2,1,0:T(8,128)}, s32[]{:T(128)}) %tuple.38), condition=%wide.while_cond, body=%wide.while_body.sunk | while | flops 2 | bytes 132205 | solution.py:46
  279.6 2.0 bitcast_dynamic-update-slice_fusion.2
  282.3 2.0 bitcast_dynamic-update-slice_fusion.2
  285.0 2.0 bitcast_dynamic-update-slice_fusion.2
  287.7 2.1 bitcast_dynamic-update-slice_fusion.2
  289.7 40.1 %custom-call.33 = f32[4,128,128]{1,2,0:T(8,128)S(1)} custom-call(f32[4,128,128]{2,1,0:T(8,128)} %get-tuple-element.9), custom_call_target="InvertDiagBlocksLowerTriangular" | custom-call | tf_op jit(solution)/shard_map/triangular_solve | solution.py:46
  333.7 8.8 %convolution_convert_fusion = bf16[8192,512]{1,0:T(8,128)(2,1)S(1)} fusion(bf16[8192,512]{1,0:T(8,128)(2,1)} %all-gather.2.cloned.1.call-done, bf16[128,512]{1,0:T(8,128)(2,1)S(1)} %convolution_convert_fusion.1, bf16[128,512]{1,0:T(8,128)(2,1)S(1)} %get-tuple-element.40, bf16[128,512]{1,0:T(8,128)(2,1)S(1)} %get-tuple-element.42, ...), kind=kOutput, calls=%fused_computation.2 | convolution fusion | flops 4301258752 | bytes 17301504 | tf_op jit(solution)/shard_map/dot_general | solution.py:63
  342.9 3.6 collective-permute-start.2
  346.5 1.6 collective-permute-start.3
  348.1 3.4 fusion.51
  353.7 3.5 fusion.52
  357.2 10.1 %convert_bitcast_fusion = bf16[32,256,128]{1,2,0:T(8,128)(2,1)} fusion(bf16[32,256,256]{2,1,0:T(8,128)(2,1)} %param.9, f32[32,128,256]{2,1,0:T(8,128)} %fusion.52, f32[32,128,256]{2,1,0:T(8,128)} %fusion.51, bf16[32,256,128]{2,1,0:T(8,128)(2,1)S(1)} %bitcast.100, bf16[32,256,256]{2,1,0:T(8,128)(2,1)} %param.6), kind=kOutput, calls=%fused_computation.13 | convolution fusion | flops 1077936128 | bytes 20971520 | tf_op jit(solution)/shard_map/bij,bjc->bic/dot_general | solution.py:39
  367.3 3.2 copy.12
  370.5 6.4 %fusion.53 = f32[512,128]{1,0:T(8,128)} fusion(bf16[8192,512]{1,0:T(8,128)(2,1)} %copy-done.5, bf16[8192,128]{1,0:T(8,128)(2,1)S(1)} %bitcast.104), kind=kOutput, calls=%fused_computation.101 | convolution fusion | flops 1073741824 | bytes 10747904 | tf_op jit(solution)/shard_map/dot_general | solution.py:21
  376.9 72.2 %all-reduce.6.cloned.1.call-done = f32[512,128]{1,0:T(8,128)} async-done(((f32[512,128]{1,0:T(8,128)}), f32[512,128]{1,0:T(8,128)}) %all-reduce.6.cloned.1.call-update) | async-done | bytes 262160 | tf_op jit(solution)/shard_map/psum | solution.py:66
  449.1 1.7 copy.31
  (67 shorter events, 20.3 us)
Async XLA Ops:
  7.2 95.2 %all-gather.2.cloned.1.call-start = ((), (), s32[]{:S(2)}) async-start(), calls=%async_computation | async-start | bytes 10485760 | tf_op jit(solution)/shard_map/all_gather | solution.py:59
  8.1 13.3 %collective-permute-start.1 = (bf16[256,128]{1,0:T(8,128)(2,1)S(1)}, bf16[256,128]{1,0:T(8,128)(2,1)S(1)}, u32[]{:S(2)}, u32[]{:S(2)}) collective-permute-start(bf16[256,128]{1,0:T(8,128)(2,1)S(1)} %get-tuple-element.26), channel_id=1, source_target_pairs={{4,0},{8,4},{12,8},{16,12},{20,16},{24,20},{28,24},{5,1},{9,5},{13... | collective-permute-start | bytes 196616 | tf_op jit(solution)/shard_map/ppermute | solution.py:15
  9.4 12.0 %collective-permute-start = (bf16[256,128]{1,0:T(8,128)(2,1)S(1)}, bf16[256,128]{1,0:T(8,128)(2,1)S(1)}, u32[]{:S(2)}, u32[]{:S(2)}) collective-permute-start(bf16[256,128]{1,0:T(8,128)(2,1)S(1)} %get-tuple-element.27), channel_id=1, source_target_pairs={{0,4},{4,8},{8,12},{12,16},{16,20},{20,24},{24,28},{1,5},{5,9},{9,... | collective-permute-start | bytes 196616 | tf_op jit(solution)/shard_map/ppermute | solution.py:12
  14.9 6.5 %copy-start.4 = (bf16[8192,128]{1,0:T(8,128)(2,1)S(1)}, bf16[8192,128]{1,0:T(8,128)(2,1)}, u32[]{:S(2)}) copy-start(bf16[8192,128]{1,0:T(8,128)(2,1)} %param.5) | copy-start | bytes 6291460
  21.4 2.2 copy-start.2
  41.2 150.9 %all-reduce.4.cloned.1.call-start = ((), (), s32[]{:S(2)}) async-start(), calls=%async_computation.1 | async-start | bytes 2097152 | tf_op jit(solution)/shard_map/psum | solution.py:60
  113.7 335.5 %all-reduce.6.cloned.1.call-start = ((), (), s32[]{:S(2)}) async-start(), calls=%async_computation.2 | async-start | bytes 524288 | tf_op jit(solution)/shard_map/psum | solution.py:66
  342.5 9.0 %copy-start.5 = (bf16[8192,512]{1,0:T(8,128)(2,1)}, bf16[8192,512]{1,0:T(8,128)(2,1)S(1)}, u32[]{:S(2)}) copy-start(bf16[8192,512]{1,0:T(8,128)(2,1)S(1)} %convolution_convert_fusion) | copy-start | bytes 25165828
  342.5 5.6 %copy-start.3 = (bf16[32,256,256]{2,1,0:T(8,128)(2,1)S(1)}, bf16[32,256,256]{2,1,0:T(8,128)(2,1)}, u32[]{:S(2)}) copy-start(bf16[32,256,256]{2,1,0:T(8,128)(2,1)} %param.7) | copy-start | bytes 12582916
  342.8 9.9 %copy-start = (bf16[8192,128]{1,0:T(8,128)(2,1)}, bf16[8192,128]{1,0:T(8,128)(2,1)S(1)}, u32[]{:S(2)}) copy-start(bf16[8192,128]{1,0:T(8,128)(2,1)S(1)} %constant_dynamic-slice_fusion.2) | copy-start | bytes 6291460
  342.9 8.7 %collective-permute-start.2 = (bf16[256,128]{1,0:T(8,128)(2,1)S(1)}, bf16[256,128]{1,0:T(8,128)(2,1)S(1)}, u32[]{:S(2)}, u32[]{:S(2)}) collective-permute-start(bf16[256,128]{1,0:T(8,128)(2,1)S(1)} %get-tuple-element.20), channel_id=1, source_target_pairs={{0,4},{4,8},{8,12},{12,16},{16,20},{20,24},{24,28},{1,5},{5,9},{9,... | collective-permute-start | bytes 196616 | tf_op jit(solution)/shard_map/ppermute | solution.py:12
  346.5 6.3 %collective-permute-start.3 = (bf16[256,128]{1,0:T(8,128)(2,1)S(1)}, bf16[256,128]{1,0:T(8,128)(2,1)S(1)}, u32[]{:S(2)}, u32[]{:S(2)}) collective-permute-start(bf16[256,128]{1,0:T(8,128)(2,1)S(1)} %get-tuple-element.21), channel_id=1, source_target_pairs={{4,0},{8,4},{12,8},{16,12},{20,16},{24,20},{28,24},{5,1},{9,5},{13... | collective-permute-start | bytes 196616 | tf_op jit(solution)/shard_map/ppermute | solution.py:15
  351.5 2.2 copy-start.1
Sparse Core Ops, SparseCore 0:
  41.3 61.0 all-gather.1
  113.8 78.2 all-reduce.3
  377.1 72.0 all-reduce.5
where the time goes:
time: 465 us; the launch traced here: 458 us
  waiting for transfers between devices  212 us (46%)
  other arithmetic  122 us (26%)
  matrix products  69.1 us (15%)
  local copies, waits for them, and re-layouts  25.2 us (5%)
  between operations  16.9 us (4%)
  starting transfers between devices  12.3 us (3%)
    another operation x14, other arithmetic, inverse_upper(): factor = jnp.linalg.cholesky(gram)  79 us
    psum x1, waiting for transfers between devices, shards(): gram = lax.psum(inner(wide, wide), 'rows')  77.2 us
    psum x1, waiting for transfers between devices, shards(): projected = lax.psum(inner(ortho_all, image), 'rows')  72.2 us
    all_gather x1, waiting for transfers between devices, shards(): wide = lax.all_gather(work, 'cols', axis=1, tiled=True)  61.1 us
    another operation x3, other arithmetic, inverse_upper(): lax.linalg.triangular_solve(factor, identity, left_side=True, lower=True)  40.3 us
    dot_general x2, matrix products, apply_blocks(): jnp.einsum('bij,bjc->bic', inverse, mixed, preferred_element_type=jnp.flo...  20.1 us
    dot_general x2, matrix products, inner(): lax.dot_general(left, right, (((0,), (0,)), ((), ())), preferred_element_...  17.7 us
    another operation x12, local copies, waits for them, and re-layouts  10.8 us
  transfers between devices with their start and end apart: 7, of which 4 were waited for; matrix products, arithmetic and copies ran while one was open for 2% of the time, Pallas kernels for 0%

commit v1 on v0

--- a/solution.py
+++ b/solution.py
@@ -56,7 +56,12 @@
         return apply_blocks(padded, lower, diag, upper, inverse)
 
     work = operate(basis)
-    wide = lax.all_gather(work, "cols", axis=1, tiled=True)
+    ring = [work]
+    for hop in range(3):
+        ring.append(lax.ppermute(ring[-1], "cols", [(dev, (dev + 1) % 4) for dev in range(4)]))
+    wide = jnp.roll(
+        jnp.concatenate(ring[::-1], axis=1), (lax.axis_index("cols") + 1) * ring[0].shape[1], axis=1
+    )
     gram = lax.psum(inner(wide, wide), "rows")
     rinv = inverse_upper(gram)
     start = lax.axis_index("cols") * width

time: 465 us -> 503 us (1.082)
  local copies, waits for them, and re-layouts: 25.2 us -> 44.2 us
  waiting for transfers between devices: 212 us -> 229 us
    ppermute x0 -> x3, waiting for transfers between devices: none -> 76.8 us  [shards(): lax.ppermute(ring[-1], 'cols', [(dev, (dev + 1) % 4) for dev in range(4)])]
    all_gather x1 -> x0, waiting for transfers between devices: 61.1 us -> none  [shards(): wide = lax.all_gather(work, 'cols', axis=1, tiled=True)]
    unnamed x13 -> x24, local copies, waits for them, and re-layouts: 4.26 us -> 23.2 us
  transfers between devices with their start and end apart: 7 -> 9, of which waited for: 4 -> 6; matrix products, arithmetic and copies ran while one was open for 2% -> 2% of each run, Pallas kernels for 0% -> 0%
where the time goes in v1:
time: 503 us; the launch traced here: 494 us
  waiting for transfers between devices  229 us (46%)
  other arithmetic  122 us (24%)
  matrix products  69.6 us (14%)
  local copies, waits for them, and re-layouts  44.2 us (9%)
  between operations  17 us (3%)
  starting transfers between devices  12.3 us (2%)
    psum x1, waiting for transfers between devices, shards(): gram = lax.psum(inner(wide, wide), 'rows')  79 us
    another operation x14, other arithmetic, inverse_upper(): factor = jnp.linalg.cholesky(gram)  79 us
    ppermute x3, waiting for transfers between devices, shards(): lax.ppermute(ring[-1], 'cols', [(dev, (dev + 1) % 4) for dev in range(4)])  76.8 us
    psum x1, waiting for transfers between devices, shards(): projected = lax.psum(inner(ortho_all, image), 'rows')  72.2 us
    another operation x3, other arithmetic, inverse_upper(): lax.linalg.triangular_solve(factor, identity, left_side=True, lower=True)  40.3 us
    unnamed x24, local copies, waits for them, and re-layouts  23.2 us
    dot_general x2, matrix products, apply_blocks(): jnp.einsum('bij,bjc->bic', inverse, mixed, preferred_element_type=jnp.flo...  20.2 us
    dot_general x2, matrix products, inner(): lax.dot_general(left, right, (((0,), (0,)), ((), ())), preferred_element_...  18 us
  transfers between devices with their start and end apart: 9, of which 6 were waited for; matrix products, arithmetic and copies ran while one was open for 2% of the time, Pallas kernels for 0%

profile of v1, /device:TPU:0, one launch (start us, length us, event | category | flops | bytes accessed | tf_op | source)
XLA Modules:
  0.0 494.5 jit_solution(10446334319870662669)
XLA Ops:
  9.4 5.5 %collective-permute-start = (bf16[256,128]{1,0:T(8,128)(2,1)S(1)}, bf16[256,128]{1,0:T(8,128)(2,1)S(1)}, u32[]{:S(2)}, u32[]{:S(2)}) collective-permute-start(bf16[256,128]{1,0:T(8,128)(2,1)S(1)} %get-tuple-element.27), channel_id=1, source_target_pairs={{0,4},{4,8},{8,12},{12,16},{16,20},{20,24},{24,28},{1,5},{5,9},{9,... | collective-permute-start | bytes 196616 | tf_op jit(solution)/shard_map/ppermute | solution.py:12
  14.9 6.5 %fusion.54 = f32[32,256,128]{1,2,0:T(8,128)} fusion(bf16[32,256,256]{2,1,0:T(8,128)(2,1)} %param.7, bf16[32,256,128]{2,1,0:T(8,128)(2,1)} %bitcast.98), kind=kOutput, calls=%fused_computation.110 | convolution fusion | flops 536870912 | bytes 10485760 | tf_op jit(solution)/shard_map/bij,bjc->bic/dot_general | solution.py:32
  23.6 3.5 fusion.53
  27.1 10.1 %convert_bitcast_fusion.1 = bf16[32,256,128]{1,2,0:T(8,128)(2,1)} fusion(bf16[32,256,256]{2,1,0:T(8,128)(2,1)} %param.9, f32[32,256,128]{1,2,0:T(8,128)} %fusion.54, f32[32,128,256]{2,1,0:T(8,128)} %fusion.53, bf16[32,256,128]{2,1,0:T(8,128)(2,1)S(1)} %bitcast.99, bf16[32,256,256]{2,1,0:T(8,128)(2,1)} %param.8), kind=kOutput, calls=%fused_computation.17 | convolution fusion | flops 1077936128 | bytes 20971520 | tf_op jit(solution)/shard_map/bij,bjc->bic/dot_general | solution.py:39
  37.1 3.2 copy.9
  40.4 25.4 %collective-permute-done.2 = bf16[8192,128]{1,0:T(8,128)(2,1)S(1)} collective-permute-done((bf16[8192,128]{1,0:T(8,128)(2,1)S(1)}, bf16[8192,128]{1,0:T(8,128)(2,1)S(1)}, u32[]{:S(2)}, u32[]{:S(2)}) %collective-permute-start.2) | collective-permute-done | bytes 2097184 | tf_op jit(solution)/shard_map/ppermute | solution.py:61
  67.2 25.6 %collective-permute-done.3 = bf16[8192,128]{1,0:T(8,128)(2,1)} collective-permute-done((bf16[8192,128]{1,0:T(8,128)(2,1)S(1)}, bf16[8192,128]{1,0:T(8,128)(2,1)}, u32[]{:S(2)}, u32[]{:S(2)}) %collective-permute-start.3) | collective-permute-done | bytes 2097184 | tf_op jit(solution)/shard_map/ppermute | solution.py:61
  92.7 25.8 %collective-permute-done.4 = bf16[8192,128]{1,0:T(8,128)(2,1)} collective-permute-done((bf16[8192,128]{1,0:T(8,128)(2,1)}, bf16[8192,128]{1,0:T(8,128)(2,1)}, u32[]{:S(2)}, u32[]{:S(2)}) %collective-permute-start.4) | collective-permute-done | bytes 2097184 | tf_op jit(solution)/shard_map/ppermute | solution.py:61
  118.5 3.2 constant_dynamic-update-slice_fusion.7
  121.7 3.3 constant_dynamic-update-slice_fusion.6
  128.2 3.1 constant_dynamic-update-slice_fusion.3
  131.3 3.2 constant_dynamic-update-slice_fusion.2
  137.7 11.6 %fusion.1 = f32[512,512]{0,1:T(8,128)} fusion(bf16[8192,1024]{1,0:T(8,128)(2,1)} %constant_dynamic-update-slice_fusion, s32[]{:T(128)S(6)} %select_n.21), kind=kOutput, calls=%fused_computation.4 | convolution fusion | flops 4294967296 | bytes 9437188 | tf_op jit(solution)/shard_map/dot_general | solution.py:21
  150.4 79.0 %all-reduce.4.cloned.1.call-done = f32[512,512]{0,1:T(8,128)} async-done(((f32[512,512]{0,1:T(8,128)}), f32[512,512]{0,1:T(8,128)}) %all-reduce.4.cloned.1.call-update) | async-done | bytes 1048592 | tf_op jit(solution)/shard_map/psum | solution.py:65
  232.5 11.7 %cholesky.104 = f32[128,128]{1,0:T(8,128)S(1)} custom-call(f32[128,128]{1,0:T(8,128)S(1)} %cholesky.266), custom_call_target="Cholesky" | custom-call | tf_op jit(solution)/shard_map/jit(cholesky)/cholesky | solution.py:44
  244.4 9.8 %custom-call.30 = f32[1,128,128]{1,2,0:T(8,128)S(1)} custom-call(f32[1,128,128]{2,1,0:T(8,128)S(1)} %get-tuple-element.37), custom_call_target="InvertDiagBlocksLowerTriangular" | custom-call | tf_op jit(solution)/shard_map/jit(cholesky)/cholesky | solution.py:44
  254.9 11.7 %cholesky.217 = f32[128,128]{1,0:T(8,128)S(1)} custom-call(f32[128,128]{1,0:T(8,128)S(1)} %cholesky.270), custom_call_target="Cholesky" | custom-call | tf_op jit(solution)/shard_map/jit(cholesky)/cholesky | solution.py:44
  266.6 10.0 %custom-call.31 = f32[1,128,128]{1,2,0:T(8,128)S(1)} custom-call(f32[1,128,128]{2,1,0:T(8,128)S(1)} %get-tuple-element.34), custom_call_target="InvertDiagBlocksLowerTriangular" | custom-call | tf_op jit(solution)/shard_map/jit(cholesky)/cholesky | solution.py:44
  277.3 11.7 %cholesky.238 = f32[128,128]{1,0:T(8,128)S(1)} custom-call(f32[128,128]{1,0:T(8,128)S(1)} %cholesky.275), custom_call_target="Cholesky" | custom-call | tf_op jit(solution)/shard_map/jit(cholesky)/cholesky | solution.py:44
  289.0 9.8 %custom-call.32 = f32[1,128,128]{1,2,0:T(8,128)S(1)} custom-call(f32[1,128,128]{2,1,0:T(8,128)S(1)} %get-tuple-element.31), custom_call_target="InvertDiagBlocksLowerTriangular" | custom-call | tf_op jit(solution)/shard_map/jit(cholesky)/cholesky | solution.py:44
  299.4 11.7 %cholesky.255 = f32[128,128]{1,0:T(8,128)S(1)} custom-call(f32[128,128]{1,0:T(8,128)S(1)} %convolution_subtract_fusion.5), custom_call_target="Cholesky" | custom-call | tf_op jit(solution)/shard_map/jit(cholesky)/cholesky | solution.py:44
  316.1 10.1 %while.1 = (s32[]{:T(128)}, f32[512,512]{1,0:T(8,128)S(1)}, s32[4,2]{0,1:T(2,128)S(1)}, f32[4,128,128]{2,1,0:T(8,128)}, s32[]{:T(128)}) while((s32[]{:T(128)}, f32[512,512]{1,0:T(8,128)S(1)}, s32[4,2]{0,1:T(2,128)S(1)}, f32[4,128,128]{2,1,0:T(8,128)}, s32[]{:T(128)}) %tuple.38), condition=%wide.while_cond, body=%wide.while_body.sunk | while | flops 2 | bytes 132205 | solution.py:46
  319.3 1.9 bitcast_dynamic-update-slice_fusion.2
  326.2 40.1 %custom-call.33 = f32[4,128,128]{1,2,0:T(8,128)S(1)} custom-call(f32[4,128,128]{2,1,0:T(8,128)} %get-tuple-element.9), custom_call_target="InvertDiagBlocksLowerTriangular" | custom-call | tf_op jit(solution)/shard_map/triangular_solve | solution.py:46
  370.2 8.8 %convolution_convert_fusion = bf16[8192,512]{1,0:T(8,128)(2,1)S(1)} fusion(bf16[8192,1024]{1,0:T(8,128)(2,1)} %constant_dynamic-update-slice_fusion, s32[]{:T(128)S(6)} %select_n.21, bf16[128,512]{1,0:T(8,128)(2,1)S(1)} %convolution_convert_fusion.1, bf16[128,512]{1,0:T(8,128)(2,1)S(1)} %get-tuple-element.40, bf16[128,512]{1,0:T(8,128)(2,1)S(1)} %get-tuple-element.42, ...), kind=kOutput, calls=%fused_computation.2 | convolution fusion | flops 4301258752 | bytes 17301508 | tf_op jit(solution)/shard_map/dot_general | solution.py:68
  379.4 3.6 collective-permute-start.5
  384.6 3.5 fusion.55
  390.3 3.5 fusion.56
  393.7 10.1 %convert_bitcast_fusion = bf16[32,256,128]{1,2,0:T(8,128)(2,1)} fusion(bf16[32,256,256]{2,1,0:T(8,128)(2,1)} %param.9, f32[32,128,256]{2,1,0:T(8,128)} %fusion.56, f32[32,128,256]{2,1,0:T(8,128)} %fusion.55, bf16[32,256,128]{2,1,0:T(8,128)(2,1)S(1)} %bitcast.100, bf16[32,256,256]{2,1,0:T(8,128)(2,1)} %param.6), kind=kOutput, calls=%fused_computation.16 | convolution fusion | flops 1077936128 | bytes 20971520 | tf_op jit(solution)/shard_map/bij,bjc->bic/dot_general | solution.py:39
  403.9 3.2 copy.12
  407.1 6.4 %fusion.57 = f32[512,128]{1,0:T(8,128)} fusion(bf16[8192,512]{1,0:T(8,128)(2,1)} %copy-done.7, bf16[8192,128]{1,0:T(8,128)(2,1)S(1)} %bitcast.103), kind=kOutput, calls=%fused_computation.113 | convolution fusion | flops 1073741824 | bytes 10747904 | tf_op jit(solution)/shard_map/dot_general | solution.py:21
  413.5 72.2 %all-reduce.6.cloned.1.call-done = f32[512,128]{1,0:T(8,128)} async-done(((f32[512,128]{1,0:T(8,128)}), f32[512,128]{1,0:T(8,128)}) %all-reduce.6.cloned.1.call-update) | async-done | bytes 262160 | tf_op jit(solution)/shard_map/psum | solution.py:71
  (82 shorter events, 38.6 us)
Async XLA Ops:
  7.2 222.3 %all-reduce.4.cloned.1.call-start = ((), (), s32[]{:S(2)}) async-start(), calls=%async_computation | async-start | bytes 2097152 | tf_op jit(solution)/shard_map/psum | solution.py:65
  8.1 13.3 %collective-permute-start.1 = (bf16[256,128]{1,0:T(8,128)(2,1)S(1)}, bf16[256,128]{1,0:T(8,128)(2,1)S(1)}, u32[]{:S(2)}, u32[]{:S(2)}) collective-permute-start(bf16[256,128]{1,0:T(8,128)(2,1)S(1)} %get-tuple-element.26), channel_id=1, source_target_pairs={{4,0},{8,4},{12,8},{16,12},{20,16},{24,20},{28,24},{5,1},{9,5},{13... | collective-permute-start | bytes 196616 | tf_op jit(solution)/shard_map/ppermute | solution.py:15
  9.4 12.0 %collective-permute-start = (bf16[256,128]{1,0:T(8,128)(2,1)S(1)}, bf16[256,128]{1,0:T(8,128)(2,1)S(1)}, u32[]{:S(2)}, u32[]{:S(2)}) collective-permute-start(bf16[256,128]{1,0:T(8,128)(2,1)S(1)} %get-tuple-element.27), channel_id=1, source_target_pairs={{0,4},{4,8},{8,12},{12,16},{16,20},{20,24},{24,28},{1,5},{5,9},{9,... | collective-permute-start | bytes 196616 | tf_op jit(solution)/shard_map/ppermute | solution.py:12
  14.9 6.5 %copy-start.4 = (bf16[8192,128]{1,0:T(8,128)(2,1)S(1)}, bf16[8192,128]{1,0:T(8,128)(2,1)}, u32[]{:S(2)}) copy-start(bf16[8192,128]{1,0:T(8,128)(2,1)} %param.5) | copy-start | bytes 6291460
  21.4 2.2 copy-start.2
  40.3 25.5 %collective-permute-start.2 = (bf16[8192,128]{1,0:T(8,128)(2,1)S(1)}, bf16[8192,128]{1,0:T(8,128)(2,1)S(1)}, u32[]{:S(2)}, u32[]{:S(2)}) collective-permute-start(bf16[8192,128]{1,0:T(8,128)(2,1)S(1)} %bitcast.95), channel_id=1, source_target_pairs={{0,1},{1,2},{2,3},{3,0},{4,5},{5,6},{6,7},{7,4},{8,9},{9,10},{10,1... | collective-permute-start | bytes 6291464 | tf_op jit(solution)/shard_map/ppermute | solution.py:61
  65.9 1.3 copy-start.5
  67.2 25.6 %collective-permute-start.3 = (bf16[8192,128]{1,0:T(8,128)(2,1)S(1)}, bf16[8192,128]{1,0:T(8,128)(2,1)}, u32[]{:S(2)}, u32[]{:S(2)}) collective-permute-start(bf16[8192,128]{1,0:T(8,128)(2,1)S(1)} %collective-permute-done.2), channel_id=1, source_target_pairs={{0,1},{1,2},{2,3},{3,0},{4,5},{5,6},{6,7},{7,4},{8,9},{9,10},{10,1... | collective-permute-start | bytes 6291464 | tf_op jit(solution)/shard_map/ppermute | solution.py:61
  92.7 25.8 %collective-permute-start.4 = (bf16[8192,128]{1,0:T(8,128)(2,1)}, bf16[8192,128]{1,0:T(8,128)(2,1)}, u32[]{:S(2)}, u32[]{:S(2)}) collective-permute-start(bf16[8192,128]{1,0:T(8,128)(2,1)} %collective-permute-done.3), channel_id=1, source_target_pairs={{0,1},{1,2},{2,3},{3,0},{4,5},{5,6},{6,7},{7,4},{8,9},{9,10},{10,1... | collective-permute-start | bytes 6291464 | tf_op jit(solution)/shard_map/ppermute | solution.py:61
  92.7 32.2 %copy-start.6 = (bf16[8192,128]{1,0:T(8,128)(2,1)S(1)}, bf16[8192,128]{1,0:T(8,128)(2,1)}, u32[]{:S(2)}) copy-start(bf16[8192,128]{1,0:T(8,128)(2,1)} %copy-done.5) | copy-start | bytes 6291460
  149.3 336.5 %all-reduce.6.cloned.1.call-start = ((), (), s32[]{:S(2)}) async-start(), calls=%async_computation.1 | async-start | bytes 524288 | tf_op jit(solution)/shard_map/psum | solution.py:71
  379.0 9.0 %copy-start.7 = (bf16[8192,512]{1,0:T(8,128)(2,1)}, bf16[8192,512]{1,0:T(8,128)(2,1)S(1)}, u32[]{:S(2)}) copy-start(bf16[8192,512]{1,0:T(8,128)(2,1)S(1)} %convolution_convert_fusion) | copy-start | bytes 25165828
  379.1 5.6 %copy-start.3 = (bf16[32,256,256]{2,1,0:T(8,128)(2,1)S(1)}, bf16[32,256,256]{2,1,0:T(8,128)(2,1)}, u32[]{:S(2)}) copy-start(bf16[32,256,256]{2,1,0:T(8,128)(2,1)} %param.7) | copy-start | bytes 12582916
  379.4 9.9 %copy-start = (bf16[8192,128]{1,0:T(8,128)(2,1)}, bf16[8192,128]{1,0:T(8,128)(2,1)S(1)}, u32[]{:S(2)}) copy-start(bf16[8192,128]{1,0:T(8,128)(2,1)S(1)} %constant_dynamic-slice_fusion.2) | copy-start | bytes 6291460
  379.4 8.7 %collective-permute-start.5 = (bf16[256,128]{1,0:T(8,128)(2,1)S(1)}, bf16[256,128]{1,0:T(8,128)(2,1)S(1)}, u32[]{:S(2)}, u32[]{:S(2)}) collective-permute-start(bf16[256,128]{1,0:T(8,128)(2,1)S(1)} %get-tuple-element.20), channel_id=1, source_target_pairs={{0,4},{4,8},{8,12},{12,16},{16,20},{20,24},{24,28},{1,5},{5,9},{9,... | collective-permute-start | bytes 196616 | tf_op jit(solution)/shard_map/ppermute | solution.py:12
  383.0 6.3 %collective-permute-start.6 = (bf16[256,128]{1,0:T(8,128)(2,1)S(1)}, bf16[256,128]{1,0:T(8,128)(2,1)S(1)}, u32[]{:S(2)}, u32[]{:S(2)}) collective-permute-start(bf16[256,128]{1,0:T(8,128)(2,1)S(1)} %get-tuple-element.21), channel_id=1, source_target_pairs={{4,0},{8,4},{12,8},{16,12},{20,16},{24,20},{28,24},{5,1},{9,5},{13... | collective-permute-start | bytes 196616 | tf_op jit(solution)/shard_map/ppermute | solution.py:15
  388.1 2.2 copy-start.1
Sparse Core Ops, SparseCore 0:
  149.4 79.9 all-reduce.3
  413.7 72.0 all-reduce.5
